TPU v7x, 256 devices: a whole 4x4x8 slice. The times are simulated.
256 devices in a mesh: freq: 8 (over x, z_lo), trial: 32 (over y, z_hi, core).
Axes of the slice: x: 4, y: 4, z: 8 (z_hi: 4, z_lo: 2; z = z_hi * 2 + z_lo), core: 2. Of those that a mesh axis runs over, the one named last changes fastest.
Arguments:
- signals: bfloat16 [64, 306, 1024], P('trial'), may hold values from -6 to 6
- kernel: bfloat16 [8192, 306], P('trial'), may hold values from -0.3125 to 0.3125
- freqs: float32 [40], P('freq'), may hold values from 3.6 to 66
Outputs:
- rel_power: float32 [8192, 640], P('trial', 'freq')
- itc_score: float32 [8192, 640], P('trial', 'freq')
All inputs are finite; a program needn't handle non-finite values.
Results may differ from a plain program's by a relative error of at most 0.0003.
Values may be sent and summed in bfloat16 or wider, within the bound.
No kernel may reach another device: no remote copies, remote signals or barrier semaphores. Data moves between devices by JAX's collectives and lax.ppermute only.
A program may use at most 64 MiB of HBM per device.

v0:
```python
import jax
import jax.numpy as jnp
from jax import lax
from jax.sharding import PartitionSpec as P

TOUT = 16


CYCLES = 7.0
SAMPLE_RATE = 1000.0
PHASE_FLOOR = 0.25
MEAN_EPSILON = 1e-06


def from_partner(value, axis, distance):
    return lax.ppermute(value, axis, [(i, i ^ 1 << distance) for i in range(lax.axis_size(axis))])


def copy_for_each(value, axis):
    length = lax.axis_size(axis)
    return lax.all_to_all(
        jnp.broadcast_to(value[None], (length, *value.shape)), axis, 0, 0, tiled=True
    )


def over_copies(value, axis):
    return copy_for_each(value, axis).sum(axis=0)


def wavelet_table(frequencies, sample_count, point_count):
    stride = sample_count // point_count
    moments = jnp.arange(sample_count, dtype=frequencies.dtype)[:, None, None]
    centres = (jnp.arange(point_count, dtype=frequencies.dtype) * stride + stride // 2)[
        None, None, :
    ]
    widths = CYCLES * SAMPLE_RATE / (2.0 * jnp.pi) / frequencies[None, :, None]
    offset = moments - centres
    envelope = jnp.exp(-offset * offset / (2.0 * widths * widths)) * (8.0 / widths)
    angles = 2.0 * jnp.pi / SAMPLE_RATE * frequencies[None, :, None] * offset
    stacked = jnp.stack([envelope * jnp.cos(angles), envelope * jnp.sin(angles)], axis=1)
    return stacked.reshape(sample_count, -1)


def source_terms(kernel_rows, coefficients, span):
    source = jnp.einsum(
        "sc,ncm->snm",
        kernel_rows.astype(jnp.float32),
        coefficients,
        precision=lax.Precision.HIGHEST,
        preferred_element_type=jnp.float32,
    )
    real_part = source[:, :, :span]
    imag_part = source[:, :, span:]
    magnitude = real_part * real_part + imag_part * imag_part
    inverse = lax.rsqrt(magnitude + PHASE_FLOOR)
    return jnp.concatenate(
        [
            jnp.sum(magnitude, axis=1),
            jnp.sum(real_part * inverse, axis=1),
            jnp.sum(imag_part * inverse, axis=1),
        ],
        axis=1,
    )


def shards(signals, kernel, freqs):
    trial_count, chan_count, sample_count = signals.shape
    span = freqs.shape[0] * TOUT
    table = wavelet_table(freqs, sample_count, TOUT)
    flat = signals.reshape(trial_count * chan_count, sample_count)
    coefficients = jnp.dot(
        flat, table, precision=lax.Precision.HIGHEST, preferred_element_type=jnp.float32
    )
    coefficients = coefficients.reshape(trial_count, chan_count, 2 * span)
    all_trials = trial_count * lax.axis_size("trial")
    owned_rows = kernel.shape[0]
    position = lax.axis_index("trial")
    bit_total = lax.axis_size("trial").bit_length() - 1
    group_trials = coefficients
    for level in range(2):
        partner = from_partner(group_trials, "trial", level)
        group_trials = jnp.concatenate([group_trials, partner], axis=0)
    blocks = kernel[None]
    for level in range(2, bit_total):
        other = from_partner(blocks, "trial", level)
        upper = position >> level & 1 == 1
        blocks = jnp.where(
            upper, jnp.stack([other, blocks], axis=0), jnp.stack([blocks, other], axis=0)
        )
        blocks = blocks.reshape((-1,) + kernel.shape)
    kernel_quarter = blocks.reshape(-1, chan_count)
    partials = source_terms(kernel_quarter, group_trials, span)
    partials = partials.reshape((-1, owned_rows, 3 * span))
    for level in range(bit_total - 1, 1, -1):
        halves = partials.reshape((2, -1, owned_rows, 3 * span))
        upper = position >> level & 1 == 1
        keeping = jnp.where(upper, halves[1], halves[0])
        sending = jnp.where(upper, halves[0], halves[1])
        partials = keeping + from_partner(sending, "trial", level)
    totals = partials.reshape(owned_rows, 3 * span)
    power = totals[:, :span] / all_trials
    phase_real = totals[:, span : 2 * span]
    phase_imag = totals[:, 2 * span :]
    source_sum = over_copies(jnp.sum(power, axis=1), "freq")
    mean_power = source_sum / (span * lax.axis_size("freq"))
    rel_power = power / (mean_power[:, None] + MEAN_EPSILON)
    itc_score = (phase_real * phase_real + phase_imag * phase_imag) / all_trials
    return (rel_power, itc_score)


def solution(mesh):
    placed = (P("trial", None, None), P("trial", None), P("freq"))
    return jax.shard_map(
        shards,
        mesh=mesh,
        in_specs=placed,
        out_specs=(P("trial", "freq"), P("trial", "freq")),
        check_vma=False,
    )
```

profile of v0, /device:TPU:8, one launch (start us, length us, event | category | flops | bytes accessed | tf_op | source)
XLA Modules:
  0.0 150.7 jit_solution(16979999540881119691)
XLA Ops:
  0.6 7.3 %collective-permute-start = (bf16[1,256,306]{1,2,0:T(8,128)(2,1)}, bf16[1,256,306]{1,2,0:T(8,128)(2,1)S(1)}, u32[]{:S(2)}, u32[]{:S(2)}) collective-permute-start(bf16[1,256,306]{1,2,0:T(8,128)(2,1)} %bitcast.36), channel_id=1, source_target_pairs={{0,4},{1,5},{2,6},{3,7},{4,0},{5,1},{6,2},{7,3},{8,12},{9,13},{10,... | collective-permute-start | bytes 470024 | tf_op jit(solution)/shard_map/ppermute | solution.py:16
  7.9 0.7 multiply_multiply_fusion
  8.7 1.3 fusion.1
  9.9 1.6 %copy.37 = bf16[2,306,1024]{2,1,0:T(8,128)(2,1)S(1)} copy(bf16[2,306,1024]{2,0,1:T(2,128)(2,1)} %param.3) | data formatting | bytes 2506752 | tf_op args[0]
  12.5 0.8 maximum_select_fusion.2
  13.3 0.4 collective-permute-start.1
  13.7 1.3 convolution_bitcast_fusion
  15.6 1.0 maximum_select_fusion.3
  16.6 5.9 %collective-permute-done.1 = bf16[2,256,306]{1,2,0:T(8,128)(2,1)} collective-permute-done((bf16[2,256,306]{1,2,0:T(8,128)(2,1)}, bf16[2,256,306]{1,2,0:T(8,128)(2,1)}, u32[]{:S(2)}, u32[]{:S(2)}) %collective-permute-start.1) | collective-permute-done | bytes 313376 | tf_op jit(solution)/shard_map/ppermute | solution.py:16
  22.6 1.2 maximum_select_fusion.1
  24.0 2.4 %collective-permute-start.2 = (bf16[4,256,306]{1,0,2:T(4,128)(2,1)S(1)}, bf16[4,256,306]{1,0,2:T(4,128)(2,1)S(1)}, u32[]{:S(2)}, u32[]{:S(2)}) collective-permute-start(bf16[4,256,306]{1,0,2:T(4,128)(2,1)S(1)} %copy.42), channel_id=1, source_target_pairs={{0,16},{1,17},{2,18},{3,19},{4,20},{5,21},{6,22},{7,23},{8,24},{9,... | collective-permute-start | bytes 1880072 | tf_op jit(solution)/shard_map/ppermute | solution.py:16
  26.4 1.0 pad_maximum_fusion.2
  27.4 4.7 %collective-permute-start.4 = (f32[4,306,160]{1,2,0:T(8,128)}, f32[4,306,160]{1,2,0:T(8,128)}, u32[]{:S(2)}, u32[]{:S(2)}) collective-permute-start(f32[4,306,160]{1,2,0:T(8,128)} %pad_maximum_fusion.2), channel_id=1, source_target_pairs={{0,2},{1,3},{2,0},{3,1},{4,6},{5,7},{6,4},{7,5},{8,10},{9,11},{10,... | collective-permute-start | bytes 2350088 | tf_op jit(solution)/shard_map/ppermute | solution.py:16
  32.4 7.9 %collective-permute-done.2 = bf16[4,256,306]{1,0,2:T(4,128)(2,1)S(1)} collective-permute-done((bf16[4,256,306]{1,0,2:T(4,128)(2,1)S(1)}, bf16[4,256,306]{1,0,2:T(4,128)(2,1)S(1)}, u32[]{:S(2)}, u32[]{:S(2)}) %collective-permute-start.2) | collective-permute-done | bytes 626720 | tf_op jit(solution)/shard_map/ppermute | solution.py:16
  40.3 0.9 maximum_select_fusion
  41.3 0.4 copy.36
  41.7 0.8 select_n.111
  42.5 31.1 %collective-permute-done.4 = f32[4,306,160]{1,2,0:T(8,128)} collective-permute-done((f32[4,306,160]{1,2,0:T(8,128)}, f32[4,306,160]{1,2,0:T(8,128)}, u32[]{:S(2)}, u32[]{:S(2)}) %collective-permute-start.4) | collective-permute-done | bytes 783392 | tf_op jit(solution)/shard_map/ppermute | solution.py:16
  73.5 1.3 pad_maximum_fusion
  74.9 8.3 %fusion.9 = f32[2048,1280]{0,1:S(1)} fusion(bf16[2048,306]{0,1:T(8,128)(2,1)S(1)} %select_n.111, f32[306,1280]{0,1:T(8,128)S(1)} %bitcast.30), kind=kOutput, calls=%fused_computation.42 | convolution fusion | flops 9625927680 | bytes 13305856
  83.2 2.2 %fusion.8 = (f32[2048,80]{0,1:T(8,128)S(1)}, f32[2048,80]{0,1:T(8,128)S(1)}, f32[2048,80]{0,1:T(8,128)S(1)}) fusion(f32[2048,8,160]{0,2,1:T(8,128)S(1)} %bitcast.29), kind=kLoop, calls=%fused_computation.41 | loop fusion | flops 11304960 | bytes 12451840 | tf_op jit(solution)/shard_map/reduce_sum | solution.py:58
  85.7 0.5 select_n.115
  86.2 1.3 collective-permute-start.5
  87.5 0.5 select_n.113
  88.0 22.8 %collective-permute-done.5 = f32[4,256,240]{1,0,2:T(4,128)} collective-permute-done((f32[4,256,240]{1,0,2:T(4,128)S(1)}, f32[4,256,240]{1,0,2:T(4,128)}, u32[]{:S(2)}, u32[]{:S(2)}) %collective-permute-start.5) | collective-permute-done | bytes 983072 | tf_op jit(solution)/shard_map/ppermute | solution.py:16
  110.7 1.5 add.45
  112.5 1.4 collective-permute-start.6
  113.9 10.1 %collective-permute-done.6 = f32[2,256,240]{1,0,2:T(2,128)S(1)} collective-permute-done((f32[2,256,240]{1,0,2:T(2,128)S(1)}, f32[2,256,240]{1,0,2:T(2,128)S(1)}, u32[]{:S(2)}, u32[]{:S(2)}) %collective-permute-start.6) | collective-permute-done | bytes 491552 | tf_op jit(solution)/shard_map/ppermute | solution.py:16
  124.7 4.6 %collective-permute-start.7 = (f32[1,256,240]{1,0,2:T(1,128)S(1)}, f32[1,256,240]{1,0,2:T(1,128)S(1)}, u32[]{:S(2)}, u32[]{:S(2)}) collective-permute-start(f32[1,256,240]{1,0,2:T(1,128)S(1)} %broadcast_select_fusion.1), channel_id=1, source_target_pairs={{0,4},{1,5},{2,6},{3,7},{4,0},{5,1},{6,2},{7,3},{8,12},{9,13},{10,... | collective-permute-start | bytes 737288 | tf_op jit(solution)/shard_map/ppermute | solution.py:16
  129.3 9.9 %collective-permute-done.7 = f32[1,256,240]{1,0,2:T(1,128)S(1)} collective-permute-done((f32[1,256,240]{1,0,2:T(1,128)S(1)}, f32[1,256,240]{1,0,2:T(1,128)S(1)}, u32[]{:S(2)}, u32[]{:S(2)}) %collective-permute-start.7) | collective-permute-done | bytes 245792 | tf_op jit(solution)/shard_map/ppermute | solution.py:16
  139.7 10.3 %all_to_all.6 = f32[8,1,256]{2,1,0:T(1,128)S(1)} all-to-all(f32[8,1,256]{2,1,0:T(1,128)S(1)} %broadcast_in_dim.5), channel_id=1, replica_groups=mesh['freq'=8,'trial'=32] {'freq'}, dimensions={0} | all-to-all | bytes 16384 | tf_op jit(solution)/shard_map/all_to_all | solution.py:21
  150.0 0.7 fusion.5
  (28 shorter events, 3.6 us)
Async XLA Ops:
  0.6 11.7 %collective-permute-start = (bf16[1,256,306]{1,2,0:T(8,128)(2,1)}, bf16[1,256,306]{1,2,0:T(8,128)(2,1)S(1)}, u32[]{:S(2)}, u32[]{:S(2)}) collective-permute-start(bf16[1,256,306]{1,2,0:T(8,128)(2,1)} %bitcast.36), channel_id=1, source_target_pairs={{0,4},{1,5},{2,6},{3,7},{4,0},{5,1},{6,2},{7,3},{8,12},{9,13},{10,... | collective-permute-start | bytes 470024 | tf_op jit(solution)/shard_map/ppermute | solution.py:16
  11.6 0.9 copy-start
  12.5 2.9 %copy-start.2 = (bf16[1,256,306]{1,2,0:T(8,128)(2,1)}, bf16[1,256,306]{1,2,0:T(8,128)(2,1)S(1)}, u32[]{:S(2)}) copy-start(bf16[1,256,306]{1,2,0:T(8,128)(2,1)S(1)} %collective-permute-done) | copy-start | bytes 470020
  13.3 9.3 %collective-permute-start.1 = (bf16[2,256,306]{1,2,0:T(8,128)(2,1)}, bf16[2,256,306]{1,2,0:T(8,128)(2,1)}, u32[]{:S(2)}, u32[]{:S(2)}) collective-permute-start(bf16[2,256,306]{1,2,0:T(8,128)(2,1)} %maximum_select_fusion.2), channel_id=1, source_target_pairs={{0,8},{1,9},{2,10},{3,11},{4,12},{5,13},{6,14},{7,15},{8,0},{9,1},... | collective-permute-start | bytes 940040 | tf_op jit(solution)/shard_map/ppermute | solution.py:16
  13.7 1.9 %copy-start.1 = (bf16[256,306]{0,1:T(8,128)(2,1)S(1)}, bf16[256,306]{0,1:T(8,128)(2,1)}, u32[]{:S(2)}) copy-start(bf16[256,306]{0,1:T(8,128)(2,1)} %param.4) | copy-start | bytes 470020
  15.5 10.9 %collective-permute-start.3 = (f32[2,306,160]{1,2,0:T(8,128)S(1)}, f32[2,306,160]{1,2,0:T(8,128)S(1)}, u32[]{:S(2)}, u32[]{:S(2)}) collective-permute-start(f32[2,306,160]{1,2,0:T(8,128)S(1)} %copy.40), channel_id=1, source_target_pairs={{0,1},{1,0},{2,3},{3,2},{4,5},{5,4},{6,7},{7,6},{8,9},{9,8},{10,11... | collective-permute-start | bytes 1175048 | tf_op jit(solution)/shard_map/ppermute | solution.py:16
  24.0 16.3 %collective-permute-start.2 = (bf16[4,256,306]{1,0,2:T(4,128)(2,1)S(1)}, bf16[4,256,306]{1,0,2:T(4,128)(2,1)S(1)}, u32[]{:S(2)}, u32[]{:S(2)}) collective-permute-start(bf16[4,256,306]{1,0,2:T(4,128)(2,1)S(1)} %copy.42), channel_id=1, source_target_pairs={{0,16},{1,17},{2,18},{3,19},{4,20},{5,21},{6,22},{7,23},{8,24},{9,... | collective-permute-start | bytes 1880072 | tf_op jit(solution)/shard_map/ppermute | solution.py:16
  27.4 46.1 %collective-permute-start.4 = (f32[4,306,160]{1,2,0:T(8,128)}, f32[4,306,160]{1,2,0:T(8,128)}, u32[]{:S(2)}, u32[]{:S(2)}) collective-permute-start(f32[4,306,160]{1,2,0:T(8,128)} %pad_maximum_fusion.2), channel_id=1, source_target_pairs={{0,2},{1,3},{2,0},{3,1},{4,6},{5,7},{6,4},{7,5},{8,10},{9,11},{10,... | collective-permute-start | bytes 2350088 | tf_op jit(solution)/shard_map/ppermute | solution.py:16
  86.2 24.5 %collective-permute-start.5 = (f32[4,256,240]{1,0,2:T(4,128)S(1)}, f32[4,256,240]{1,0,2:T(4,128)}, u32[]{:S(2)}, u32[]{:S(2)}) collective-permute-start(f32[4,256,240]{1,0,2:T(4,128)S(1)} %select_n.115), channel_id=1, source_target_pairs={{0,16},{1,17},{2,18},{3,19},{4,20},{5,21},{6,22},{7,23},{8,24},{9,... | collective-permute-start | bytes 2949128 | tf_op jit(solution)/shard_map/ppermute | solution.py:16
  112.5 11.5 %collective-permute-start.6 = (f32[2,256,240]{1,0,2:T(2,128)S(1)}, f32[2,256,240]{1,0,2:T(2,128)S(1)}, u32[]{:S(2)}, u32[]{:S(2)}) collective-permute-start(f32[2,256,240]{1,0,2:T(2,128)S(1)} %broadcast_select_fusion), channel_id=1, source_target_pairs={{0,8},{1,9},{2,10},{3,11},{4,12},{5,13},{6,14},{7,15},{8,0},{9,1},... | collective-permute-start | bytes 1474568 | tf_op jit(solution)/shard_map/ppermute | solution.py:16
  124.7 14.6 %collective-permute-start.7 = (f32[1,256,240]{1,0,2:T(1,128)S(1)}, f32[1,256,240]{1,0,2:T(1,128)S(1)}, u32[]{:S(2)}, u32[]{:S(2)}) collective-permute-start(f32[1,256,240]{1,0,2:T(1,128)S(1)} %broadcast_select_fusion.1), channel_id=1, source_target_pairs={{0,4},{1,5},{2,6},{3,7},{4,0},{5,1},{6,2},{7,3},{8,12},{9,13},{10,... | collective-permute-start | bytes 737288 | tf_op jit(solution)/shard_map/ppermute | solution.py:16
where the time goes:
time: 154 us; the launch traced here: 151 us
  waiting for transfers between devices  88.2 us (57%)
  starting transfers between devices  22.3 us (14%)
  other arithmetic  14.3 us (9%)
  blocking collectives  10.3 us (7%)
  matrix products  9.64 us (6%)
  local copies, waits for them, and re-layouts  5.09 us (3%)
    ppermute x8, waiting for transfers between devices, from_partner(): lax.ppermute(value, axis, [(i, i ^ 1 << distance) for i in range(lax.axis...  88.2 us
    ppermute x8, starting transfers between devices, from_partner(): lax.ppermute(value, axis, [(i, i ^ 1 << distance) for i in range(lax.axis...  22.3 us
    all_to_all x1, blocking collectives, copy_for_each(): lax.all_to_all(jnp.broadcast_to(value[None], (length, *value.shape)), axi...  10.3 us
    unnamed x1, matrix products  8.32 us
    select_n x4, other arithmetic, shards(): jnp.where(upper, jnp.stack([other, blocks], axis=0), jnp.stack([blocks, o...  3.92 us
  transfers between devices with their start and end apart: 8, of which 7 were waited for; matrix products, arithmetic and copies ran while one was open for 8% of the time, Pallas kernels for 0%

commit v1 on v0

v1 whole, which is shorter than its diff:
```python
import jax
import jax.numpy as jnp
from jax import lax
from jax.experimental import pallas as pl
from jax.experimental.pallas import tpu as pltpu
from jax.sharding import PartitionSpec as P

TOUT = 16
CYCLES = 7.0
SAMPLE_RATE = 1000.0
PHASE_FLOOR = 0.25
MEAN_EPSILON = 1e-06

LEVELS = 30000.0
STEPS = 128.0
CENTRE = 120.0

BOTH = ("freq", "trial")


def place_of(index):
    freq, trial = divmod(index, 32)
    return freq // 2, freq % 2, trial // 8, trial // 2 % 4, trial % 2


def index_of(x, z_lo, y, z_hi, core):
    return (x * 2 + z_lo) * 32 + y * 8 + z_hi * 2 + core


def moved(value, rule):
    count = lax.axis_size("freq") * lax.axis_size("trial")
    return lax.ppermute(value, BOTH, [(i, index_of(*rule(*place_of(i)))) for i in range(count)])


def along_y(step):
    return lambda x, zl, y, zh, c: (x, zl, (y + step) % 4, zh, c)


def other_core(x, zl, y, zh, c):
    return x, zl, y, zh, 1 - c


def next_pair(x, zl, y, zh, c):
    return x, 1 - zl, y, (zh + (1 if zl else -1)) % 4, c


def same_pair(x, zl, y, zh, c):
    return x, 1 - zl, y, zh, c


def near(x, zl, y, zh, c):
    return x, zl, y, (zh + (1 if zl else -1)) % 4, c


def far(x, zl, y, zh, c):
    return x, zl, y, (zh + (-1 if zl else 1)) % 4, c


def opposite(x, zl, y, zh, c):
    return x, zl, y, (zh + 2) % 4, c


def encoded(level):
    size = jnp.abs(level)
    octave = jnp.floor(size * (1.0 / STEPS))
    value = (1.0 + (size - octave * STEPS) * (1.0 / STEPS)) * jnp.exp2(octave - CENTRE)
    return jnp.where(level < 0.0, -value, value).astype(jnp.bfloat16)


def decoded(code):
    value = code.astype(jnp.float32)
    size = jnp.abs(value)
    octave = jnp.floor(jnp.log2(size))
    level = STEPS * (octave + (CENTRE - 1.0)) + STEPS * size * jnp.exp2(-octave)
    return jnp.where(value < 0.0, -level, level)


def split(value):
    high = value.astype(jnp.bfloat16)
    return high, (value - high.astype(jnp.float32)).astype(jnp.bfloat16)


def nt(a, b):
    return lax.dot_general(a, b, (((1,), (1,)), ((), ())), preferred_element_type=jnp.float32)


def lanes_of(shape):
    return lax.broadcasted_iota(jnp.int32, shape, 1)


def coefficients_body(signals, waves, wire, shifts, table, rest):
    samples = signals.shape[2]
    span = table.shape[0] // 4
    tail = signals.shape[1] - 256
    length = waves.shape[1]
    stride = samples // TOUT
    waves = waves[...]
    turned = pltpu.roll(waves, length - stride, 1)
    for point in range(TOUT):
        start = samples - stride * (point + 1)
        part = waves if start % 128 == 0 else turned
        start -= start % 128
        for cut in range(0, samples, 128):
            piece = part[:, start + cut : start + cut + 128]
            first = cut // 128 * 2 * span + point
            shifts[pl.ds(first, waves.shape[0], stride=TOUT), :] = piece
    for cut in range(0, samples, 128):
        first = cut // 128 * 2 * span
        high, low = split(shifts[first : first + 2 * span, :])
        table[: 2 * span, cut : cut + 128] = high
        table[2 * span :, cut : cut + 128] = low
    rest[...] = jnp.zeros(rest.shape, rest.dtype)
    rest[:tail, :] = signals[0, 256:, :]
    rest[64 : 64 + tail, :] = signals[1, 256:, :]
    both = nt(table[...], rest[...])
    ends = both[: 2 * span] + both[2 * span :]
    lane = lanes_of(ends.shape)
    first = lane < 64
    used = (lane & 63) < tail
    sizes = jnp.where(used, jnp.abs(ends), 0.0)
    scales = []
    for n in range(2):
        both = nt(table[...], signals[n, :256, :])
        main = both[: 2 * span] + both[2 * span :]
        own = jnp.where(first == (n == 0), sizes, 0.0)
        top = jnp.maximum(jnp.maximum(jnp.abs(main[:, :128]), jnp.abs(main[:, 128:])), own)
        top = jnp.max(top, axis=1, keepdims=True) * 1.01 + 1e-30
        top = top.astype(jnp.bfloat16).astype(jnp.float32)
        level = encoded(jnp.round(main * (LEVELS / top)))
        wire[n * 2 * span : (n + 1) * 2 * span, :] = level[:, :128]
        wire[(n + 2) * 2 * span : (n + 3) * 2 * span, :] = level[:, 128:]
        scales.append(top)
    scale = jnp.where(first, scales[0], scales[1])
    level = encoded(jnp.round(jnp.where(used, ends, 0.0) * (LEVELS / scale)))
    level = jnp.where((lane & 63) == tail, scale, level.astype(jnp.float32))
    wire[8 * span : 10 * span, :] = level.astype(jnp.bfloat16)


def columns_body(tail, *refs):
    wires, out = refs[:-1], refs[-1]
    for at, wire in enumerate(wires):
        span = wire.shape[0] // 10
        ends = wire[8 * span : 10 * span, :]
        raw = ends.astype(jnp.float32)
        ends = decoded(ends)
        first = lanes_of(ends.shape) < 64
        for n in range(2):
            scale = raw[:, 64 * n + tail : 64 * n + tail + 1] * (1.0 / LEVELS)
            base = (at * 2 + n) * 2 * span
            rows = slice(base, base + 2 * span)
            for half in range(2):
                start = (half * 2 + n) * 2 * span
                high, low = split(decoded(wire[start : start + 2 * span, :]) * scale)
                out[rows, half * 128 : half * 128 + 128] = high
                out[rows, 256 + half * 128 : 384 + half * 128] = low
            values = ends * scale
            if n == 1:
                values = pltpu.roll(values, 64, 1)
            high = values.astype(jnp.bfloat16).astype(jnp.float32)
            low = pltpu.roll(values - high, 64, 1)
            out[rows, 512:640] = jnp.where(first, high, low).astype(jnp.bfloat16)


def partials_body(send, *refs):
    groups, kernel, out, weights, sums = refs[:-4], refs[-4], refs[-3], refs[-2], refs[-1]
    tail = kernel.shape[0] - 256
    weights[0:256, :] = kernel[0:256, :]
    weights[256:512, :] = kernel[0:256, :]
    weights[512:640, :] = jnp.zeros((128, weights.shape[1]), weights.dtype)
    weights[512 : 512 + tail, :] = kernel[256:, :]
    weights[576 : 576 + tail, :] = kernel[256:, :]
    span = sums.shape[0] // 3
    sums[...] = jnp.zeros(sums.shape, sums.dtype)
    trials = sum(group.shape[0] for group in groups) // (2 * span)
    for group in groups:

        def step(i, carry):
            block = group[pl.ds(i * 4 * span, 4 * span), :]
            source = jnp.dot(block, weights[...], preferred_element_type=jnp.float32)
            for n in range(2):
                real = source[n * 2 * span : n * 2 * span + span]
                imag = source[n * 2 * span + span : (n + 1) * 2 * span]
                size = real * real + imag * imag
                inverse = lax.rsqrt(size + PHASE_FLOOR)
                sums[0:span, :] += size
                sums[span : 2 * span, :] += real * inverse
                sums[2 * span : 3 * span, :] += imag * inverse
            return carry

        lax.fori_loop(0, group.shape[0] // (4 * span), step, 0)
    if not send:
        out[...] = sums[...]
        return
    power = sums[0:span, :]
    top = jnp.max(power, axis=0, keepdims=True) * 1.01 + 1e-30
    top = top.astype(jnp.bfloat16)
    scale = (2.0 * LEVELS) / top.astype(jnp.float32)
    out[0:span, :] = encoded(jnp.round(power * scale - LEVELS))
    out[span : 3 * span, :] = encoded(jnp.round(sums[span : 3 * span, :] * (LEVELS / trials)))
    out[3 * span : 3 * span + 16, :] = jnp.broadcast_to(top, (16, top.shape[1]))


def totals_body(trials, all_trials, own, *refs):
    wires, power, score, sums = refs[:-3], refs[-3], refs[-2], refs[-1]
    span = power.shape[0]
    total = own[0:span, :]
    phases = own[span : 3 * span, :]
    for wire in wires:
        top = wire[3 * span : 3 * span + 16, :].astype(jnp.float32)[0:1]
        total += (decoded(wire[0:span, :]) + LEVELS) * (top * (0.5 / LEVELS))
        phases += decoded(wire[span : 3 * span, :]) * (trials / LEVELS)
    total = total * (1.0 / all_trials)
    power[...] = total
    real, imag = phases[:span], phases[span:]
    score[...] = (real * real + imag * imag) * (1.0 / all_trials)
    sums[...] = jnp.sum(total, axis=0, keepdims=True)


def scaled_body(columns, power, sums, out):
    mean = jnp.sum(sums[...], axis=0) / columns
    out[...] = power[...] / (mean + MEAN_EPSILON)


def waves_of(frequencies, sample_count):
    stride = sample_count // TOUT
    offset = jnp.arange(2 * sample_count, dtype=jnp.float32)[None, :] - (sample_count - stride // 2)
    widths = CYCLES * SAMPLE_RATE / (2.0 * jnp.pi) / frequencies[:, None]
    envelope = jnp.exp(-offset * offset / (2.0 * widths * widths)) * (8.0 / widths)
    angles = 2.0 * jnp.pi / SAMPLE_RATE * frequencies[:, None] * offset
    return jnp.concatenate([envelope * jnp.cos(angles), envelope * jnp.sin(angles)], axis=0)


def call(body, shape, dtype, *args, scratch=(), name=None):
    many = isinstance(dtype, (list, tuple))
    shapes = (
        [jax.ShapeDtypeStruct(s, d) for s, d in zip(shape, dtype)]
        if many
        else jax.ShapeDtypeStruct(shape, dtype)
    )
    return pl.pallas_call(
        body,
        out_shape=shapes,
        scratch_shapes=list(scratch),
        name=name,
    )(*args)


def shards(signals, kernel, freqs):
    trial_count, chan_count, sample_count = signals.shape
    span = freqs.shape[0] * TOUT
    rows = kernel.shape[0]
    tail = chan_count - 256
    all_trials = trial_count * lax.axis_size("trial")
    bf16, f32 = jnp.bfloat16, jnp.float32

    kernel_own = kernel.T
    kernel_near = moved(kernel_own, next_pair)
    kernel_far = moved(kernel_near, same_pair)
    kernel_opposite = moved(kernel_far, next_pair)

    wire = call(
        coefficients_body,
        (10 * span, 128),
        bf16,
        signals,
        waves_of(freqs, sample_count),
        scratch=[
            pltpu.VMEM((sample_count // 128 * 2 * span, 128), f32),
            pltpu.VMEM((4 * span, sample_count), bf16),
            pltpu.VMEM((128, sample_count), bf16),
        ],
        name="coefficients",
    )
    others = [moved(wire, along_y(step)) for step in (2, 1, -1)]
    twin = moved(wire, other_core)
    twins = [moved(other, other_core) for other in others]

    def columns(*wires):
        return call(
            lambda *refs: columns_body(tail, *refs),
            (len(wires) * 4 * span, 640),
            bf16,
            *wires,
            name="columns",
        )

    groups = [columns(wire, twin), columns(*others, *twins)]

    def partials(rows_of, send):
        return call(
            lambda *refs: partials_body(send, *refs),
            (3 * span + 16, rows) if send else (3 * span, rows),
            bf16 if send else f32,
            *groups,
            rows_of,
            scratch=[pltpu.VMEM((640, rows), bf16), pltpu.VMEM((3 * span, rows), f32)],
            name="partials",
        )

    received = [
        moved(partials(kernel_opposite, True), opposite),
        moved(partials(kernel_near, True), near),
        moved(partials(kernel_far, True), far),
    ]
    own = partials(kernel_own, False)
    trials = 8 * trial_count
    power, score, sums = call(
        lambda *refs: totals_body(trials, all_trials, *refs),
        [(span, rows), (span, rows), (1, rows)],
        [f32, f32, f32],
        own,
        *received,
        name="totals",
    )
    count = lax.axis_size("freq")
    copies = jnp.broadcast_to(sums[None], (count, 1, rows))
    sums = lax.all_to_all(copies, "freq", 0, 0, tiled=True)
    columns_in_all = float(span * count)
    rel_power = call(
        lambda *refs: scaled_body(columns_in_all, *refs),
        (span, rows),
        f32,
        power,
        sums,
        name="scaled",
    )
    return rel_power.T, score.T


def solution(mesh):
    placed = (P("trial", None, None), P("trial", None), P("freq"))
    return jax.shard_map(
        shards,
        mesh=mesh,
        in_specs=placed,
        out_specs=(P("trial", "freq"), P("trial", "freq")),
        check_vma=False,
    )
```

time: 154 us -> 85.4 us (0.55); the launches traced: 151 us -> 85 us
  waiting for transfers between devices: 88.2 us -> 10.5 us
  Pallas kernels: 0 us -> 35.4 us
  other arithmetic: 14.3 us -> 1.67 us
  matrix products: 9.64 us -> 0 us
  starting transfers between devices: 22.3 us -> 19.6 us
  local copies, waits for them, and re-layouts: 5.09 us -> 6.78 us
    ppermute x8 -> x13, waiting for transfers between devices: 88.2 us -> 10.5 us  [moved(): lax.ppermute(value, BOTH, [(i, index_of(*rule(*place_of(i)))) for i in ra...]
    pallas_call x0 -> x9, Pallas kernels: none -> 35.4 us  [call(): pl.pallas_call(body, out_shape=shapes, scratch_shapes=list(scratch), name...]
    unnamed x1 -> x0, matrix products: 8.32 us -> none
    select_n x7 -> x0, other arithmetic: 4.58 us -> none  [the longest x4 3.92 us: shards(): jnp.where(upper, jnp.stack([other, blocks], axis=0), jnp.stack([blocks, o...]
    unnamed x8 -> x27, local copies, waits for them, and re-layouts: 1.82 us -> 6.09 us
    ppermute x8 -> x13, starting transfers between devices: 22.3 us -> 19.6 us  [moved(): lax.ppermute(value, BOTH, [(i, index_of(*rule(*place_of(i)))) for i in ra...]
    select_n x6 -> x0, local copies, waits for them, and re-layouts: 2.61 us -> none  [the longest x4 1.68 us: shards(): jnp.where(upper, jnp.stack([other, blocks], axis=0), jnp.stack([blocks, o...]
    reduce_sum x3 -> x0, other arithmetic: 2.27 us -> none  [the longest x1 2.22 us: source_terms(): jnp.sum(magnitude, axis=1)]
  transfers between devices with their start and end apart: 8 -> 13, of which waited for: 7 -> 3; matrix products, arithmetic and copies ran while one was open for 8% -> 5% of each run, Pallas kernels for 0% -> 37%
where the time goes in v1:
time: 85.4 us; the launch traced here: 85 us
  Pallas kernels  35.4 us (41%)
  starting transfers between devices  19.6 us (23%)
  waiting for transfers between devices  10.5 us (12%)
  blocking collectives  10.4 us (12%)
  local copies, waits for them, and re-layouts  6.78 us (8%)
  other arithmetic  1.67 us (2%)
    pallas_call x9, Pallas kernels, call(): pl.pallas_call(body, out_shape=shapes, scratch_shapes=list(scratch), name...  35.4 us
    ppermute x13, starting transfers between devices, moved(): lax.ppermute(value, BOTH, [(i, index_of(*rule(*place_of(i)))) for i in ra...  19.6 us
    ppermute x13, waiting for transfers between devices, moved(): lax.ppermute(value, BOTH, [(i, index_of(*rule(*place_of(i)))) for i in ra...  10.5 us
    all_to_all x1, blocking collectives, shards(): sums = lax.all_to_all(copies, 'freq', 0, 0, tiled=True)  10.4 us
    unnamed x27, local copies, waits for them, and re-layouts  6.09 us
  transfers between devices with their start and end apart: 13, of which 3 were waited for; matrix products, arithmetic and copies ran while one was open for 5% of the time, Pallas kernels for 37%

profile of v1, /device:TPU:8, one launch (start us, length us, event | category | flops | bytes accessed | tf_op | source)
XLA Modules:
  0.0 85.0 jit_solution(12054577123036406370)
XLA Ops:
  0.6 5.9 %collective-permute-start.7 = (bf16[306,256]{1,0:T(8,128)(2,1)}, bf16[306,256]{1,0:T(8,128)(2,1)S(1)}, u32[]{:S(2)}, u32[]{:S(2)}) collective-permute-start(bf16[306,256]{1,0:T(8,128)(2,1)} %bitcast.4), channel_id=1, source_target_pairs={{0,38},{1,39},{2,32},{3,33},{4,34},{5,35},{6,36},{7,37},{8,46},{9,... | collective-permute-start | bytes 470024 | tf_op jit(solution)/shard_map/ppermute | solution.py:32
  6.6 0.7 multiply_multiply_fusion
  7.2 0.3 fusion.1
  7.6 0.7 pad_maximum_fusion.waves
  8.2 2.7 %copy.5.signals = bf16[2,306,1024]{2,1,0:T(8,128)(2,1)} copy(bf16[2,306,1024]{2,0,1:T(2,128)(2,1)} %param.3) | data formatting | bytes 2506752 | tf_op args[0]
  10.9 3.1 %coefficients.1.refs_0_ = bf16[800,128]{1,0:T(8,128)(2,1)} custom-call(bf16[2,306,1024]{2,1,0:T(8,128)(2,1)} %copy.5.signals, f32[10,2048]{1,0:T(8,128)} %pad_maximum_fusion.waves), custom_call_target="tpu_custom_call" | custom-call | tf_op jit(solution)/shard_map/coefficients/pallas_call | solution.py:240
  14.1 2.3 %collective-permute-start.1 = (bf16[800,128]{1,0:T(8,128)(2,1)}, bf16[800,128]{1,0:T(8,128)(2,1)S(1)}, u32[]{:S(2)}, u32[]{:S(2)}) collective-permute-start(bf16[800,128]{1,0:T(8,128)(2,1)} %coefficients.1.refs_0_), channel_id=1, source_target_pairs={{0,16},{1,17},{2,18},{3,19},{4,20},{5,21},{6,22},{7,23},{8,24},{9,... | collective-permute-start | bytes 614408 | tf_op jit(solution)/shard_map/ppermute | solution.py:32
  16.4 2.0 %collective-permute-start.3 = (bf16[800,128]{1,0:T(8,128)(2,1)}, bf16[800,128]{1,0:T(8,128)(2,1)S(1)}, u32[]{:S(2)}, u32[]{:S(2)}) collective-permute-start(bf16[800,128]{1,0:T(8,128)(2,1)} %coefficients.1.refs_0_), channel_id=1, source_target_pairs={{0,24},{1,25},{2,26},{3,27},{4,28},{5,29},{6,30},{7,31},{8,0},{9,1... | collective-permute-start | bytes 614408 | tf_op jit(solution)/shard_map/ppermute | solution.py:32
  18.4 0.1 collective-permute-start
  18.5 5.3 %collective-permute-done.1.refs_0_ = bf16[800,128]{1,0:T(8,128)(2,1)S(1)} collective-permute-done((bf16[800,128]{1,0:T(8,128)(2,1)}, bf16[800,128]{1,0:T(8,128)(2,1)S(1)}, u32[]{:S(2)}, u32[]{:S(2)}) %collective-permute-start.1) | collective-permute-done | bytes 204832 | tf_op jit(solution)/shard_map/ppermute | solution.py:32
  23.8 3.1 %collective-permute-done.2.refs_1_ = bf16[800,128]{1,0:T(8,128)(2,1)S(1)} collective-permute-done((bf16[800,128]{1,0:T(8,128)(2,1)}, bf16[800,128]{1,0:T(8,128)(2,1)S(1)}, u32[]{:S(2)}, u32[]{:S(2)}) %collective-permute-start.2) | collective-permute-done | bytes 204832 | tf_op jit(solution)/shard_map/ppermute | solution.py:32
  26.9 0.5 collective-permute-start.6
  27.4 0.3 collective-permute-start.9
  27.7 0.7 copy-done.6
  28.4 2.6 %columns.2.refs_0_ = bf16[640,640]{1,0:T(8,128)(2,1)} custom-call(bf16[800,128]{1,0:T(8,128)(2,1)} %coefficients.1.refs_0_, bf16[800,128]{1,0:T(8,128)(2,1)} %copy-done.6), custom_call_target="tpu_custom_call" | custom-call | tf_op jit(solution)/shard_map/columns/pallas_call | solution.py:240
  31.1 0.6 copy-done.3
  31.7 0.1 copy-done.4
  31.8 0.7 copy-done.5
  32.5 4.9 %columns.3.refs_1_ = bf16[1920,640]{1,0:T(8,128)(2,1)} custom-call(bf16[800,128]{1,0:T(8,128)(2,1)} %copy-done, bf16[800,128]{1,0:T(8,128)(2,1)} %copy-done.1, bf16[800,128]{1,0:T(8,128)(2,1)} %copy-done.2, bf16[800,128]{1,0:T(8,128)(2,1)} %copy-done.3, bf16[800,128]{1,0:T(8,128)(2,1)} %copy-done.4, bf16[800,128]{1,0:T(8,128)(2,1)} %copy-done.5), custom_call_target="tpu_custom_call" | custom-call | tf_op jit(solution)/shard_map/columns/pallas_call | solution.py:240
  37.4 5.2 %partials.7 = bf16[256,256]{1,0:T(8,128)(2,1)} custom-call(bf16[640,640]{1,0:T(8,128)(2,1)} %columns.2.refs_0_, bf16[1920,640]{1,0:T(8,128)(2,1)} %columns.3.refs_1_, bf16[306,256]{1,0:T(8,128)(2,1)} %copy-done.8), custom_call_target="tpu_custom_call" | custom-call | tf_op jit(solution)/shard_map/partials/pallas_call | solution.py:240
  42.6 5.2 %partials.6 = bf16[256,256]{1,0:T(8,128)(2,1)} custom-call(bf16[640,640]{1,0:T(8,128)(2,1)} %columns.2.refs_0_, bf16[1920,640]{1,0:T(8,128)(2,1)} %columns.3.refs_1_, bf16[306,256]{1,0:T(8,128)(2,1)} %copy-done.7), custom_call_target="tpu_custom_call" | custom-call | tf_op jit(solution)/shard_map/partials/pallas_call | solution.py:240
  47.9 4.1 %collective-permute-start.11 = (bf16[256,256]{1,0:T(8,128)(2,1)}, bf16[256,256]{1,0:T(8,128)(2,1)S(1)}, u32[]{:S(2)}, u32[]{:S(2)}) collective-permute-start(bf16[256,256]{1,0:T(8,128)(2,1)} %partials.6), channel_id=1, source_target_pairs={{0,6},{1,7},{2,0},{3,1},{4,2},{5,3},{6,4},{7,5},{8,14},{9,15},{10,... | collective-permute-start | bytes 393224 | tf_op jit(solution)/shard_map/ppermute | solution.py:32
  52.0 0.7 copy-done.9
  52.7 5.2 %partials.5 = bf16[256,256]{1,0:T(8,128)(2,1)} custom-call(bf16[640,640]{1,0:T(8,128)(2,1)} %columns.2.refs_0_, bf16[1920,640]{1,0:T(8,128)(2,1)} %columns.3.refs_1_, bf16[306,256]{1,0:T(8,128)(2,1)} %copy-done.9), custom_call_target="tpu_custom_call" | custom-call | tf_op jit(solution)/shard_map/partials/pallas_call | solution.py:240
  57.9 4.3 %collective-permute-start.10 = (bf16[256,256]{1,0:T(8,128)(2,1)}, bf16[256,256]{1,0:T(8,128)(2,1)S(1)}, u32[]{:S(2)}, u32[]{:S(2)}) collective-permute-start(bf16[256,256]{1,0:T(8,128)(2,1)} %partials.5), channel_id=1, source_target_pairs={{0,4},{1,5},{2,6},{3,7},{4,0},{5,1},{6,2},{7,3},{8,12},{9,13},{10,... | collective-permute-start | bytes 393224 | tf_op jit(solution)/shard_map/ppermute | solution.py:32
  62.2 5.2 %partials.4.refs_0_ = f32[240,256]{1,0:T(8,128)} custom-call(bf16[640,640]{1,0:T(8,128)(2,1)} %columns.2.refs_0_, bf16[1920,640]{1,0:T(8,128)(2,1)} %columns.3.refs_1_, bf16[306,256]{1,0:T(8,128)(2,1)} %bitcast.5), custom_call_target="tpu_custom_call" | custom-call | tf_op jit(solution)/shard_map/partials/pallas_call | solution.py:240
  67.4 2.1 %collective-permute-done.10.refs_1_ = bf16[256,256]{1,0:T(8,128)(2,1)S(1)} collective-permute-done((bf16[256,256]{1,0:T(8,128)(2,1)}, bf16[256,256]{1,0:T(8,128)(2,1)S(1)}, u32[]{:S(2)}, u32[]{:S(2)}) %collective-permute-start.10) | collective-permute-done | bytes 131104 | tf_op jit(solution)/shard_map/ppermute | solution.py:32
  69.6 0.7 copy-done.12
  70.2 2.2 %totals.1 = (f32[80,256]{1,0:T(8,128)}, f32[80,256]{1,0:T(8,128)}, f32[1,256]{1,0:T(1,128)}) custom-call(f32[240,256]{1,0:T(8,128)} %partials.4.refs_0_, bf16[256,256]{1,0:T(8,128)(2,1)} %copy-done.12, bf16[256,256]{1,0:T(8,128)(2,1)} %copy-done.11, bf16[256,256]{1,0:T(8,128)(2,1)} %copy-done.10), custom_call_target="tpu_custom_call" | custom-call | tf_op jit(solution)/shard_map/totals/pallas_call | solution.py:240
  72.4 0.7 broadcast_in_dim.5
  73.1 10.4 %all_to_all.5.refs_1_ = f32[8,1,256]{2,1,0:T(1,128)} all-to-all(f32[8,1,256]{2,1,0:T(1,128)S(1)} %broadcast_in_dim.5), channel_id=1, replica_groups=mesh['freq'=8,'trial'=32] {'freq'}, dimensions={0} | all-to-all | bytes 16384 | tf_op jit(solution)/shard_map/all_to_all | solution.py:317
  83.5 1.5 %scaled.1 = f32[80,256]{1,0:T(8,128)} custom-call(f32[80,256]{1,0:T(8,128)} %get-tuple-element.5.refs_0_, f32[8,1,256]{2,1,0:T(1,128)} %all_to_all.5.refs_1_), custom_call_target="tpu_custom_call" | custom-call | tf_op jit(solution)/shard_map/scaled/pallas_call | solution.py:240
  (36 shorter events, 0.1 us)
Async XLA Ops:
  0.6 17.8 %collective-permute-start.7 = (bf16[306,256]{1,0:T(8,128)(2,1)}, bf16[306,256]{1,0:T(8,128)(2,1)S(1)}, u32[]{:S(2)}, u32[]{:S(2)}) collective-permute-start(bf16[306,256]{1,0:T(8,128)(2,1)} %bitcast.4), channel_id=1, source_target_pairs={{0,38},{1,39},{2,32},{3,33},{4,34},{5,35},{6,36},{7,37},{8,46},{9,... | collective-permute-start | bytes 470024 | tf_op jit(solution)/shard_map/ppermute | solution.py:32
  14.1 9.7 %collective-permute-start.1 = (bf16[800,128]{1,0:T(8,128)(2,1)}, bf16[800,128]{1,0:T(8,128)(2,1)S(1)}, u32[]{:S(2)}, u32[]{:S(2)}) collective-permute-start(bf16[800,128]{1,0:T(8,128)(2,1)} %coefficients.1.refs_0_), channel_id=1, source_target_pairs={{0,16},{1,17},{2,18},{3,19},{4,20},{5,21},{6,22},{7,23},{8,24},{9,... | collective-permute-start | bytes 614408 | tf_op jit(solution)/shard_map/ppermute | solution.py:32
  16.4 10.5 %collective-permute-start.2 = (bf16[800,128]{1,0:T(8,128)(2,1)}, bf16[800,128]{1,0:T(8,128)(2,1)S(1)}, u32[]{:S(2)}, u32[]{:S(2)}) collective-permute-start(bf16[800,128]{1,0:T(8,128)(2,1)} %coefficients.1.refs_0_), channel_id=1, source_target_pairs={{0,8},{1,9},{2,10},{3,11},{4,12},{5,13},{6,14},{7,15},{8,16},{9,17... | collective-permute-start | bytes 614408 | tf_op jit(solution)/shard_map/ppermute | solution.py:32
  16.4 10.5 %collective-permute-start.3 = (bf16[800,128]{1,0:T(8,128)(2,1)}, bf16[800,128]{1,0:T(8,128)(2,1)S(1)}, u32[]{:S(2)}, u32[]{:S(2)}) collective-permute-start(bf16[800,128]{1,0:T(8,128)(2,1)} %coefficients.1.refs_0_), channel_id=1, source_target_pairs={{0,24},{1,25},{2,26},{3,27},{4,28},{5,29},{6,30},{7,31},{8,0},{9,1... | collective-permute-start | bytes 614408 | tf_op jit(solution)/shard_map/ppermute | solution.py:32
  18.4 24.2 %copy-start.7 = (bf16[306,256]{1,0:T(8,128)(2,1)}, bf16[306,256]{1,0:T(8,128)(2,1)S(1)}, u32[]{:S(2)}) copy-start(bf16[306,256]{1,0:T(8,128)(2,1)S(1)} %collective-permute-done.7.refs_2_) | copy-start | bytes 470020
  18.4 9.0 %collective-permute-start.8 = (bf16[306,256]{1,0:T(8,128)(2,1)S(1)}, bf16[306,256]{1,0:T(8,128)(2,1)S(1)}, u32[]{:S(2)}, u32[]{:S(2)}) collective-permute-start(bf16[306,256]{1,0:T(8,128)(2,1)S(1)} %collective-permute-done.7.refs_2_), channel_id=1, source_target_pairs={{0,32},{1,33},{2,34},{3,35},{4,36},{5,37},{6,38},{7,39},{8,40},{9,... | collective-permute-start | bytes 470024 | tf_op jit(solution)/shard_map/ppermute | solution.py:32
  18.4 9.3 %collective-permute-start = (bf16[800,128]{1,0:T(8,128)(2,1)}, bf16[800,128]{1,0:T(8,128)(2,1)S(1)}, u32[]{:S(2)}, u32[]{:S(2)}) collective-permute-start(bf16[800,128]{1,0:T(8,128)(2,1)} %coefficients.1.refs_0_), channel_id=1, source_target_pairs={{0,1},{1,0},{2,3},{3,2},{4,5},{5,4},{6,7},{7,6},{8,9},{9,8},{10,11... | collective-permute-start | bytes 614408 | tf_op jit(solution)/shard_map/ppermute | solution.py:32
  23.8 7.3 %copy-start = (bf16[800,128]{1,0:T(8,128)(2,1)}, bf16[800,128]{1,0:T(8,128)(2,1)S(1)}, u32[]{:S(2)}) copy-start(bf16[800,128]{1,0:T(8,128)(2,1)S(1)} %collective-permute-done.1.refs_0_) | copy-start | bytes 614404
  23.8 7.2 %collective-permute-start.4 = (bf16[800,128]{1,0:T(8,128)(2,1)S(1)}, bf16[800,128]{1,0:T(8,128)(2,1)S(1)}, u32[]{:S(2)}, u32[]{:S(2)}) collective-permute-start(bf16[800,128]{1,0:T(8,128)(2,1)S(1)} %collective-permute-done.1.refs_0_), channel_id=1, source_target_pairs={{0,1},{1,0},{2,3},{3,2},{4,5},{5,4},{6,7},{7,6},{8,9},{9,8},{10,11... | collective-permute-start | bytes 614408 | tf_op jit(solution)/shard_map/ppermute | solution.py:32
  26.9 4.2 %copy-start.1 = (bf16[800,128]{1,0:T(8,128)(2,1)}, bf16[800,128]{1,0:T(8,128)(2,1)S(1)}, u32[]{:S(2)}) copy-start(bf16[800,128]{1,0:T(8,128)(2,1)S(1)} %collective-permute-done.2.refs_1_) | copy-start | bytes 614404
  26.9 4.1 %collective-permute-start.5 = (bf16[800,128]{1,0:T(8,128)(2,1)S(1)}, bf16[800,128]{1,0:T(8,128)(2,1)S(1)}, u32[]{:S(2)}, u32[]{:S(2)}) collective-permute-start(bf16[800,128]{1,0:T(8,128)(2,1)S(1)} %collective-permute-done.2.refs_1_), channel_id=1, source_target_pairs={{0,1},{1,0},{2,3},{3,2},{4,5},{5,4},{6,7},{7,6},{8,9},{9,8},{10,11... | collective-permute-start | bytes 614408 | tf_op jit(solution)/shard_map/ppermute | solution.py:32
  26.9 4.2 %copy-start.2 = (bf16[800,128]{1,0:T(8,128)(2,1)}, bf16[800,128]{1,0:T(8,128)(2,1)S(1)}, u32[]{:S(2)}) copy-start(bf16[800,128]{1,0:T(8,128)(2,1)S(1)} %collective-permute-done.3.refs_2_) | copy-start | bytes 614404
  26.9 4.1 %collective-permute-start.6 = (bf16[800,128]{1,0:T(8,128)(2,1)S(1)}, bf16[800,128]{1,0:T(8,128)(2,1)S(1)}, u32[]{:S(2)}, u32[]{:S(2)}) collective-permute-start(bf16[800,128]{1,0:T(8,128)(2,1)S(1)} %collective-permute-done.3.refs_2_), channel_id=1, source_target_pairs={{0,1},{1,0},{2,3},{3,2},{4,5},{5,4},{6,7},{7,6},{8,9},{9,8},{10,11... | collective-permute-start | bytes 614408 | tf_op jit(solution)/shard_map/ppermute | solution.py:32
  27.4 10.0 %copy-start.8 = (bf16[306,256]{1,0:T(8,128)(2,1)}, bf16[306,256]{1,0:T(8,128)(2,1)S(1)}, u32[]{:S(2)}) copy-start(bf16[306,256]{1,0:T(8,128)(2,1)S(1)} %collective-permute-done.8.refs_2_) | copy-start | bytes 470020
  27.4 24.6 %collective-permute-start.9 = (bf16[306,256]{1,0:T(8,128)(2,1)S(1)}, bf16[306,256]{1,0:T(8,128)(2,1)S(1)}, u32[]{:S(2)}, u32[]{:S(2)}) collective-permute-start(bf16[306,256]{1,0:T(8,128)(2,1)S(1)} %collective-permute-done.8.refs_2_), channel_id=1, source_target_pairs={{0,38},{1,39},{2,32},{3,33},{4,34},{5,35},{6,36},{7,37},{8,46},{9,... | collective-permute-start | bytes 470024 | tf_op jit(solution)/shard_map/ppermute | solution.py:32
  27.7 0.7 copy-start.6
  31.0 0.7 copy-start.3
  31.0 0.8 copy-start.4
  31.8 0.7 copy-start.5
  42.6 24.8 %collective-permute-start.12 = (bf16[256,256]{1,0:T(8,128)(2,1)}, bf16[256,256]{1,0:T(8,128)(2,1)S(1)}, u32[]{:S(2)}, u32[]{:S(2)}) collective-permute-start(bf16[256,256]{1,0:T(8,128)(2,1)} %partials.7), channel_id=1, source_target_pairs={{0,2},{1,3},{2,4},{3,5},{4,6},{5,7},{6,0},{7,1},{8,10},{9,11},{10,... | collective-permute-start | bytes 393224 | tf_op jit(solution)/shard_map/ppermute | solution.py:32
  47.9 19.5 %collective-permute-start.11 = (bf16[256,256]{1,0:T(8,128)(2,1)}, bf16[256,256]{1,0:T(8,128)(2,1)S(1)}, u32[]{:S(2)}, u32[]{:S(2)}) collective-permute-start(bf16[256,256]{1,0:T(8,128)(2,1)} %partials.6), channel_id=1, source_target_pairs={{0,6},{1,7},{2,0},{3,1},{4,2},{5,3},{6,4},{7,5},{8,14},{9,15},{10,... | collective-permute-start | bytes 393224 | tf_op jit(solution)/shard_map/ppermute | solution.py:32
  52.0 0.7 copy-start.9
  57.9 11.6 %collective-permute-start.10 = (bf16[256,256]{1,0:T(8,128)(2,1)}, bf16[256,256]{1,0:T(8,128)(2,1)S(1)}, u32[]{:S(2)}, u32[]{:S(2)}) collective-permute-start(bf16[256,256]{1,0:T(8,128)(2,1)} %partials.5), channel_id=1, source_target_pairs={{0,4},{1,5},{2,6},{3,7},{4,0},{5,1},{6,2},{7,3},{8,12},{9,13},{10,... | collective-permute-start | bytes 393224 | tf_op jit(solution)/shard_map/ppermute | solution.py:32
  67.4 2.2 %copy-start.10 = (bf16[256,256]{1,0:T(8,128)(2,1)}, bf16[256,256]{1,0:T(8,128)(2,1)S(1)}, u32[]{:S(2)}) copy-start(bf16[256,256]{1,0:T(8,128)(2,1)S(1)} %collective-permute-done.12.refs_3_) | copy-start | bytes 393220
  67.4 2.2 %copy-start.11 = (bf16[256,256]{1,0:T(8,128)(2,1)}, bf16[256,256]{1,0:T(8,128)(2,1)S(1)}, u32[]{:S(2)}) copy-start(bf16[256,256]{1,0:T(8,128)(2,1)S(1)} %collective-permute-done.11.refs_2_) | copy-start | bytes 393220
  69.6 0.7 copy-start.12

commit v2 on v1

--- a/solution.py
+++ b/solution.py
@@ -88,10 +88,11 @@
     return lax.broadcasted_iota(jnp.int32, shape, 1)
 
 
-def coefficients_body(signals, waves, wire, shifts, table, rest):
+def coefficients_body(signals, waves, wire, shifts, table, sides):
     samples = signals.shape[2]
     span = table.shape[0] // 4
-    tail = signals.shape[1] - 256
+    tail = signals.shape[0] - 256
+    side = sides.shape[0] // 2
     length = waves.shape[1]
     stride = samples // TOUT
     waves = waves[...]
@@ -109,29 +110,34 @@
         high, low = split(shifts[first : first + 2 * span, :])
         table[: 2 * span, cut : cut + 128] = high
         table[2 * span :, cut : cut + 128] = low
-    rest[...] = jnp.zeros(rest.shape, rest.dtype)
-    rest[:tail, :] = signals[0, 256:, :]
-    rest[64 : 64 + tail, :] = signals[1, 256:, :]
-    both = nt(table[...], rest[...])
-    ends = both[: 2 * span] + both[2 * span :]
-    lane = lanes_of(ends.shape)
+    chans = signals.shape[0]
+    merged = signals[...].reshape(2 * chans, samples)
+    for at, columns in enumerate((slice(0, 128), slice(128, 2 * span))):
+        lows = slice(2 * span + columns.start, 2 * span + columns.stop)
+        found = nt(merged, table[columns, :]) + nt(merged, table[lows, :])
+        sides[at * side : at * side + 2 * chans, : columns.stop - columns.start] = found
+    lane = lanes_of((2 * span, 128))
     first = lane < 64
-    used = (lane & 63) < tail
-    sizes = jnp.where(used, jnp.abs(ends), 0.0)
-    scales = []
+    used = lane < tail
+    scales, ends = [], []
     for n in range(2):
-        both = nt(table[...], signals[n, :256, :])
-        main = both[: 2 * span] + both[2 * span :]
-        own = jnp.where(first == (n == 0), sizes, 0.0)
-        top = jnp.maximum(jnp.maximum(jnp.abs(main[:, :128]), jnp.abs(main[:, 128:])), own)
+        parts = []
+        for at in range(2):
+            part = sides[pl.ds(at * side + n, side // 2, stride=2), :]
+            parts.append(part.T[: min(2 * span - 128 * at, 128), :])
+        values = jnp.concatenate(parts, axis=0)
+        main = values[:, :256]
+        end = jnp.where(used, values[:, 256:384], 0.0)
+        top = jnp.maximum(jnp.maximum(jnp.abs(main[:, :128]), jnp.abs(main[:, 128:])), jnp.abs(end))
         top = jnp.max(top, axis=1, keepdims=True) * 1.01 + 1e-30
         top = top.astype(jnp.bfloat16).astype(jnp.float32)
         level = encoded(jnp.round(main * (LEVELS / top)))
         wire[n * 2 * span : (n + 1) * 2 * span, :] = level[:, :128]
         wire[(n + 2) * 2 * span : (n + 3) * 2 * span, :] = level[:, 128:]
         scales.append(top)
+        ends.append(jnp.round(end * (LEVELS / top)))
+    level = encoded(jnp.where(first, ends[0], pltpu.roll(ends[1], 64, 1)))
     scale = jnp.where(first, scales[0], scales[1])
-    level = encoded(jnp.round(jnp.where(used, ends, 0.0) * (LEVELS / scale)))
     level = jnp.where((lane & 63) == tail, scale, level.astype(jnp.float32))
     wire[8 * span : 10 * span, :] = level.astype(jnp.bfloat16)
 
@@ -162,41 +168,48 @@
 
 
 def partials_body(send, *refs):
-    groups, kernel, out, weights, sums = refs[:-4], refs[-4], refs[-3], refs[-2], refs[-1]
+    groups, kernel, out, weights, sources = refs[:-4], refs[-4], refs[-3], refs[-2], refs[-1]
     tail = kernel.shape[0] - 256
     weights[0:256, :] = kernel[0:256, :]
     weights[256:512, :] = kernel[0:256, :]
     weights[512:640, :] = jnp.zeros((128, weights.shape[1]), weights.dtype)
     weights[512 : 512 + tail, :] = kernel[256:, :]
     weights[576 : 576 + tail, :] = kernel[256:, :]
-    span = sums.shape[0] // 3
-    sums[...] = jnp.zeros(sums.shape, sums.dtype)
-    trials = sum(group.shape[0] for group in groups) // (2 * span)
+    at = 0
     for group in groups:
-
-        def step(i, carry):
-            block = group[pl.ds(i * 4 * span, 4 * span), :]
-            source = jnp.dot(block, weights[...], preferred_element_type=jnp.float32)
-            for n in range(2):
-                real = source[n * 2 * span : n * 2 * span + span]
-                imag = source[n * 2 * span + span : (n + 1) * 2 * span]
-                size = real * real + imag * imag
-                inverse = lax.rsqrt(size + PHASE_FLOOR)
-                sums[0:span, :] += size
-                sums[span : 2 * span, :] += real * inverse
-                sums[2 * span : 3 * span, :] += imag * inverse
-            return carry
-
-        lax.fori_loop(0, group.shape[0] // (4 * span), step, 0)
+        count = group.shape[0]
+        sources[at : at + count, :] = jnp.dot(
+            group[...], weights[...], preferred_element_type=jnp.float32
+        )
+        at += count
+    span = groups[0].shape[0] // 4
+    trials = at // (2 * span)
+    powers = []
+    for start in range(0, span, 8):
+        power = phase_real = phase_imag = 0.0
+        for n in range(trials):
+            real = sources[n * 2 * span + start : n * 2 * span + start + 8, :]
+            imag = sources[n * 2 * span + span + start : n * 2 * span + span + start + 8, :]
+            size = real * real + imag * imag
+            inverse = lax.rsqrt(size + PHASE_FLOOR)
+            power += size
+            phase_real += real * inverse
+            phase_imag += imag * inverse
+        for part, sums in enumerate((power, phase_real, phase_imag)):
+            if send and part == 0:
+                powers.append(sums)
+                continue
+            if send:
+                sums = jnp.round(sums * (LEVELS / trials))
+            rows = slice(part * span + start, part * span + start + 8)
+            out[rows, :] = encoded(sums) if send else sums
     if not send:
-        out[...] = sums[...]
         return
-    power = sums[0:span, :]
+    power = jnp.concatenate(powers, axis=0)
     top = jnp.max(power, axis=0, keepdims=True) * 1.01 + 1e-30
     top = top.astype(jnp.bfloat16)
     scale = (2.0 * LEVELS) / top.astype(jnp.float32)
     out[0:span, :] = encoded(jnp.round(power * scale - LEVELS))
-    out[span : 3 * span, :] = encoded(jnp.round(sums[span : 3 * span, :] * (LEVELS / trials)))
     out[3 * span : 3 * span + 16, :] = jnp.broadcast_to(top, (16, top.shape[1]))
 
 
@@ -213,7 +226,7 @@
     power[...] = total
     real, imag = phases[:span], phases[span:]
     score[...] = (real * real + imag * imag) * (1.0 / all_trials)
-    sums[...] = jnp.sum(total, axis=0, keepdims=True)
+    sums[...] = jnp.broadcast_to(jnp.sum(total, axis=0, keepdims=True)[None], sums.shape)
 
 
 def scaled_body(columns, power, sums, out):
@@ -230,19 +243,19 @@
     return jnp.concatenate([envelope * jnp.cos(angles), envelope * jnp.sin(angles)], axis=0)
 
 
-def call(body, shape, dtype, *args, scratch=(), name=None):
-    many = isinstance(dtype, (list, tuple))
-    shapes = (
-        [jax.ShapeDtypeStruct(s, d) for s, d in zip(shape, dtype)]
-        if many
-        else jax.ShapeDtypeStruct(shape, dtype)
-    )
-    return pl.pallas_call(
+def call(body, outs, *args, scratch=(), name=None, final=()):
+    shapes = [
+        jax.ShapeDtypeStruct(*out) if at in final else pltpu.VMEM(*out)
+        for at, out in enumerate(outs)
+    ]
+    found = pl.pallas_call(
         body,
         out_shape=shapes,
         scratch_shapes=list(scratch),
+        compiler_params=pltpu.CompilerParams(vmem_limit_bytes=24 * 2**20),
         name=name,
     )(*args)
+    return found if len(outs) > 1 else found[0]
 
 
 def shards(signals, kernel, freqs):
@@ -260,14 +273,13 @@
 
     wire = call(
         coefficients_body,
-        (10 * span, 128),
-        bf16,
-        signals,
+        [((10 * span, 128), bf16)],
+        jnp.transpose(signals, (1, 0, 2)),
         waves_of(freqs, sample_count),
         scratch=[
             pltpu.VMEM((sample_count // 128 * 2 * span, 128), f32),
             pltpu.VMEM((4 * span, sample_count), bf16),
-            pltpu.VMEM((128, sample_count), bf16),
+            pltpu.VMEM((2 * 768, 128), f32),
         ],
         name="coefficients",
     )
@@ -278,22 +290,20 @@
     def columns(*wires):
         return call(
             lambda *refs: columns_body(tail, *refs),
-            (len(wires) * 4 * span, 640),
-            bf16,
+            [((len(wires) * 4 * span, 640), bf16)],
             *wires,
             name="columns",
         )
 
-    groups = [columns(wire, twin), columns(*others, *twins)]
+    groups = [columns(value) for value in (wire, twin, *others, *twins)]
 
     def partials(rows_of, send):
         return call(
             lambda *refs: partials_body(send, *refs),
-            (3 * span + 16, rows) if send else (3 * span, rows),
-            bf16 if send else f32,
+            [((3 * span + 16, rows), bf16) if send else ((3 * span, rows), f32)],
             *groups,
             rows_of,
-            scratch=[pltpu.VMEM((640, rows), bf16), pltpu.VMEM((3 * span, rows), f32)],
+            scratch=[pltpu.VMEM((640, rows), bf16), pltpu.VMEM((32 * span, rows), f32)],
             name="partials",
         )
 
@@ -304,25 +314,24 @@
     ]
     own = partials(kernel_own, False)
     trials = 8 * trial_count
+    count = lax.axis_size("freq")
     power, score, sums = call(
         lambda *refs: totals_body(trials, all_trials, *refs),
-        [(span, rows), (span, rows), (1, rows)],
-        [f32, f32, f32],
+        [((span, rows), f32), ((span, rows), f32), ((count, 1, rows), f32)],
         own,
         *received,
         name="totals",
+        final=(1,),
     )
-    count = lax.axis_size("freq")
-    copies = jnp.broadcast_to(sums[None], (count, 1, rows))
-    sums = lax.all_to_all(copies, "freq", 0, 0, tiled=True)
+    sums = lax.all_to_all(sums, "freq", 0, 0, tiled=True)
     columns_in_all = float(span * count)
     rel_power = call(
         lambda *refs: scaled_body(columns_in_all, *refs),
-        (span, rows),
-        f32,
+        [((span, rows), f32)],
         power,
         sums,
         name="scaled",
+        final=(0,),
     )
     return rel_power.T, score.T
 

time: 85.4 us -> 60.4 us (0.71)
  Pallas kernels: 35.4 us -> 12.7 us
  local copies, waits for them, and re-layouts: 6.78 us -> 1.3 us
  waiting for transfers between devices: 10.5 us -> 14.2 us
    pallas_call x9 -> x15, Pallas kernels: 35.4 us -> 12.7 us  [call(): pl.pallas_call(body, out_shape=shapes, scratch_shapes=list(scratch), comp...]
    unnamed x27 -> x4, local copies, waits for them, and re-layouts: 6.09 us -> 1.3 us
    ppermute x13, waiting for transfers between devices: 10.5 us -> 14.2 us  [moved(): lax.ppermute(value, BOTH, [(i, index_of(*rule(*place_of(i)))) for i in ra...]
  transfers between devices with their start and end apart: 13 -> 13, of which waited for: 3 -> 3; matrix products, arithmetic and copies ran while one was open for 5% -> 2% of each run, Pallas kernels for 37% -> 19%
where the time goes in v2:
time: 60.4 us; the launch traced here: 60.3 us
  starting transfers between devices  20 us (33%)
  waiting for transfers between devices  14.2 us (24%)
  Pallas kernels  12.7 us (21%)
  blocking collectives  10.3 us (17%)
  local copies, waits for them, and re-layouts  1.3 us (2%)
  other arithmetic  1.02 us (2%)
  between operations  0.74 us (1%)
    ppermute x13, starting transfers between devices, moved(): lax.ppermute(value, BOTH, [(i, index_of(*rule(*place_of(i)))) for i in ra...  20 us
    ppermute x13, waiting for transfers between devices, moved(): lax.ppermute(value, BOTH, [(i, index_of(*rule(*place_of(i)))) for i in ra...  14.2 us
    pallas_call x15, Pallas kernels, call(): pl.pallas_call(body, out_shape=shapes, scratch_shapes=list(scratch), comp...  12.7 us
    all_to_all x1, blocking collectives, shards(): sums = lax.all_to_all(sums, 'freq', 0, 0, tiled=True)  10.3 us
    unnamed x4, local copies, waits for them, and re-layouts  1.3 us
  transfers between devices with their start and end apart: 13, of which 3 were waited for; matrix products, arithmetic and copies ran while one was open for 2% of the time, Pallas kernels for 19%

profile of v2, /device:TPU:8, one launch (start us, length us, event | category | flops | bytes accessed | tf_op | source)
XLA Modules:
  0.0 60.3 jit_solution(12110734976187352690)
XLA Ops:
  0.6 5.9 %collective-permute-start.7 = (bf16[306,256]{1,0:T(8,128)(2,1)}, bf16[306,256]{1,0:T(8,128)(2,1)S(1)}, u32[]{:S(2)}, u32[]{:S(2)}) collective-permute-start(bf16[306,256]{1,0:T(8,128)(2,1)} %bitcast.5), channel_id=1, source_target_pairs={{0,38},{1,39},{2,32},{3,33},{4,34},{5,35},{6,36},{7,37},{8,46},{9,... | collective-permute-start | bytes 470024 | tf_op jit(solution)/shard_map/ppermute | solution.py:32
  6.6 0.7 %multiply_multiply_fusion = (f32[5]{0:T(128)S(1)}, f32[5]{0:T(128)S(1)}, f32[5]{0:T(128)S(1)}) fusion(f32[5]{0:T(128)} %param.5), kind=kLoop, calls=%fused_computation.9 | loop fusion | flops 30 | bytes 80 | tf_op jit(solution)/shard_map/mul | solution.py:241
  7.2 0.3 fusion.1
  7.6 0.0 copy-start
  7.6 1.3 %copy-done = bf16[2,306,1024]{2,0,1:T(2,128)(2,1)S(1)} copy-done((bf16[2,306,1024]{2,0,1:T(2,128)(2,1)S(1)}, bf16[2,306,1024]{2,0,1:T(2,128)(2,1)}, u32[]{:S(2)}) %copy-start) | copy-done | bytes 1253400
  8.9 2.2 %coefficients.1.refs_0_ = bf16[800,128]{1,0:T(8,128)(2,1)S(1)} custom-call(bf16[306,2,1024]{2,1,0:T(2,128)(2,1)S(1)} %bitcast.4, f32[10,2048]{1,0:T(8,128)S(1)} %pad_maximum_fusion.waves), custom_call_target="tpu_custom_call" | custom-call | tf_op jit(solution)/shard_map/coefficients/pallas_call | solution.py:251
  11.2 2.4 %collective-permute-start.1 = (bf16[800,128]{1,0:T(8,128)(2,1)S(1)}, bf16[800,128]{1,0:T(8,128)(2,1)S(1)}, u32[]{:S(2)}, u32[]{:S(2)}) collective-permute-start(bf16[800,128]{1,0:T(8,128)(2,1)S(1)} %coefficients.1.refs_0_), channel_id=1, source_target_pairs={{0,16},{1,17},{2,18},{3,19},{4,20},{5,21},{6,22},{7,23},{8,24},{9,... | collective-permute-start | bytes 614408 | tf_op jit(solution)/shard_map/ppermute | solution.py:32
  13.5 2.0 %collective-permute-start.3 = (bf16[800,128]{1,0:T(8,128)(2,1)S(1)}, bf16[800,128]{1,0:T(8,128)(2,1)S(1)}, u32[]{:S(2)}, u32[]{:S(2)}) collective-permute-start(bf16[800,128]{1,0:T(8,128)(2,1)S(1)} %coefficients.1.refs_0_), channel_id=1, source_target_pairs={{0,24},{1,25},{2,26},{3,27},{4,28},{5,29},{6,30},{7,31},{8,0},{9,1... | collective-permute-start | bytes 614408 | tf_op jit(solution)/shard_map/ppermute | solution.py:32
  15.6 5.2 %collective-permute-done.1.refs_0_ = bf16[800,128]{1,0:T(8,128)(2,1)S(1)} collective-permute-done((bf16[800,128]{1,0:T(8,128)(2,1)S(1)}, bf16[800,128]{1,0:T(8,128)(2,1)S(1)}, u32[]{:S(2)}, u32[]{:S(2)}) %collective-permute-start.1) | collective-permute-done | bytes 204832 | tf_op jit(solution)/shard_map/ppermute | solution.py:32
  20.7 3.1 %collective-permute-done.2.refs_0_ = bf16[800,128]{1,0:T(8,128)(2,1)S(1)} collective-permute-done((bf16[800,128]{1,0:T(8,128)(2,1)S(1)}, bf16[800,128]{1,0:T(8,128)(2,1)S(1)}, u32[]{:S(2)}, u32[]{:S(2)}) %collective-permute-start.2) | collective-permute-done | bytes 204832 | tf_op jit(solution)/shard_map/ppermute | solution.py:32
  23.8 0.5 collective-permute-start.6
  24.3 0.3 collective-permute-start.9
  24.7 0.4 columns.8.refs_0_
  25.1 0.4 columns.10.refs_2_
  25.5 0.4 columns.11.refs_3_
  25.9 0.4 columns.12.refs_4_
  26.3 0.4 columns.9.refs_1_
  26.7 0.4 columns.13.refs_5_
  27.1 0.4 columns.14.refs_6_
  27.5 0.4 columns.15.refs_7_
  27.9 1.5 %partials.7 = bf16[256,256]{1,0:T(8,128)(2,1)S(1)} custom-call(bf16[320,640]{1,0:T(8,128)(2,1)S(1)} %columns.8.refs_0_, bf16[320,640]{1,0:T(8,128)(2,1)S(1)} %columns.9.refs_1_, bf16[320,640]{1,0:T(8,128)(2,1)S(1)} %columns.10.refs_2_, bf16[320,640]{1,0:T(8,128)(2,1)S(1)} %columns.11.refs_3_, bf16[320,640]{1,0:T(8,128)(2,1)S(1)} %columns.12.refs_4_, ...), custom_call_target="tpu_custom_call" | custom-call | tf_op jit(solution)/shard_map/partials/pallas_call | solution.py:251
  29.4 0.3 collective-permute-start.12
  29.7 1.4 %partials.6 = bf16[256,256]{1,0:T(8,128)(2,1)S(1)} custom-call(bf16[320,640]{1,0:T(8,128)(2,1)S(1)} %columns.8.refs_0_, bf16[320,640]{1,0:T(8,128)(2,1)S(1)} %columns.9.refs_1_, bf16[320,640]{1,0:T(8,128)(2,1)S(1)} %columns.10.refs_2_, bf16[320,640]{1,0:T(8,128)(2,1)S(1)} %columns.11.refs_3_, bf16[320,640]{1,0:T(8,128)(2,1)S(1)} %columns.12.refs_4_, ...), custom_call_target="tpu_custom_call" | custom-call | tf_op jit(solution)/shard_map/partials/pallas_call | solution.py:251
  31.1 0.0 copy-start.1
  31.1 4.2 %collective-permute-start.11 = (bf16[256,256]{1,0:T(8,128)(2,1)S(1)}, bf16[256,256]{1,0:T(8,128)(2,1)S(1)}, u32[]{:S(2)}, u32[]{:S(2)}) collective-permute-start(bf16[256,256]{1,0:T(8,128)(2,1)S(1)} %partials.6), channel_id=1, source_target_pairs={{0,6},{1,7},{2,0},{3,1},{4,2},{5,3},{6,4},{7,5},{8,14},{9,15},{10,... | collective-permute-start | bytes 393224 | tf_op jit(solution)/shard_map/ppermute | solution.py:32
  35.3 1.4 %partials.5 = bf16[256,256]{1,0:T(8,128)(2,1)S(1)} custom-call(bf16[320,640]{1,0:T(8,128)(2,1)S(1)} %columns.8.refs_0_, bf16[320,640]{1,0:T(8,128)(2,1)S(1)} %columns.9.refs_1_, bf16[320,640]{1,0:T(8,128)(2,1)S(1)} %columns.10.refs_2_, bf16[320,640]{1,0:T(8,128)(2,1)S(1)} %columns.11.refs_3_, bf16[320,640]{1,0:T(8,128)(2,1)S(1)} %columns.12.refs_4_, ...), custom_call_target="tpu_custom_call" | custom-call | tf_op jit(solution)/shard_map/partials/pallas_call | solution.py:251
  36.8 4.3 %collective-permute-start.10 = (bf16[256,256]{1,0:T(8,128)(2,1)S(1)}, bf16[256,256]{1,0:T(8,128)(2,1)S(1)}, u32[]{:S(2)}, u32[]{:S(2)}) collective-permute-start(bf16[256,256]{1,0:T(8,128)(2,1)S(1)} %partials.5), channel_id=1, source_target_pairs={{0,4},{1,5},{2,6},{3,7},{4,0},{5,1},{6,2},{7,3},{8,12},{9,13},{10,... | collective-permute-start | bytes 393224 | tf_op jit(solution)/shard_map/ppermute | solution.py:32
  41.1 1.3 %partials.4.refs_0_ = f32[240,256]{1,0:T(8,128)S(1)} custom-call(bf16[320,640]{1,0:T(8,128)(2,1)S(1)} %columns.8.refs_0_, bf16[320,640]{1,0:T(8,128)(2,1)S(1)} %columns.9.refs_1_, bf16[320,640]{1,0:T(8,128)(2,1)S(1)} %columns.10.refs_2_, bf16[320,640]{1,0:T(8,128)(2,1)S(1)} %columns.11.refs_3_, bf16[320,640]{1,0:T(8,128)(2,1)S(1)} %columns.12.refs_4_, ...), custom_call_target="tpu_custom_call" | custom-call | tf_op jit(solution)/shard_map/partials/pallas_call | solution.py:251
  42.5 5.9 %collective-permute-done.10.refs_1_ = bf16[256,256]{1,0:T(8,128)(2,1)S(1)} collective-permute-done((bf16[256,256]{1,0:T(8,128)(2,1)S(1)}, bf16[256,256]{1,0:T(8,128)(2,1)S(1)}, u32[]{:S(2)}, u32[]{:S(2)}) %collective-permute-start.10) | collective-permute-done | bytes 131104 | tf_op jit(solution)/shard_map/ppermute | solution.py:32
  48.4 0.9 %totals.1 = (f32[80,256]{1,0:T(8,128)S(1)}, f32[80,256]{1,0:T(8,128)}, f32[8,1,256]{2,1,0:T(1,128)S(1)}) custom-call(f32[240,256]{1,0:T(8,128)S(1)} %partials.4.refs_0_, bf16[256,256]{1,0:T(8,128)(2,1)S(1)} %collective-permute-done.10.refs_1_, bf16[256,256]{1,0:T(8,128)(2,1)S(1)} %collective-permute-done.11.refs_2_, ...), custom_call_target="tpu_custom_call" | custom-call | tf_op jit(solution)/shard_map/totals/pallas_call | solution.py:251
  49.3 10.3 %all_to_all.5.refs_1_ = f32[8,1,256]{2,1,0:T(1,128)S(1)} all-to-all(f32[8,1,256]{2,1,0:T(1,128)S(1)} %get-tuple-element.6), channel_id=1, replica_groups=mesh['freq'=8,'trial'=32] {'freq'}, dimensions={0} | all-to-all | bytes 16384 | tf_op jit(solution)/shard_map/all_to_all | solution.py:326
  59.6 0.7 %scaled.1 = f32[80,256]{1,0:T(8,128)} custom-call(f32[80,256]{1,0:T(8,128)S(1)} %get-tuple-element.5.refs_0_, f32[8,1,256]{2,1,0:T(1,128)S(1)} %all_to_all.5.refs_1_), custom_call_target="tpu_custom_call" | custom-call | tf_op jit(solution)/shard_map/scaled/pallas_call | solution.py:251
  (18 shorter events, 0.1 us)
Async XLA Ops:
  0.6 14.9 %collective-permute-start.7 = (bf16[306,256]{1,0:T(8,128)(2,1)}, bf16[306,256]{1,0:T(8,128)(2,1)S(1)}, u32[]{:S(2)}, u32[]{:S(2)}) collective-permute-start(bf16[306,256]{1,0:T(8,128)(2,1)} %bitcast.5), channel_id=1, source_target_pairs={{0,38},{1,39},{2,32},{3,33},{4,34},{5,35},{6,36},{7,37},{8,46},{9,... | collective-permute-start | bytes 470024 | tf_op jit(solution)/shard_map/ppermute | solution.py:32
  7.6 1.3 %copy-start = (bf16[2,306,1024]{2,0,1:T(2,128)(2,1)S(1)}, bf16[2,306,1024]{2,0,1:T(2,128)(2,1)}, u32[]{:S(2)}) copy-start(bf16[2,306,1024]{2,0,1:T(2,128)(2,1)} %param.3) | copy-start | bytes 3760132
  11.2 9.6 %collective-permute-start.1 = (bf16[800,128]{1,0:T(8,128)(2,1)S(1)}, bf16[800,128]{1,0:T(8,128)(2,1)S(1)}, u32[]{:S(2)}, u32[]{:S(2)}) collective-permute-start(bf16[800,128]{1,0:T(8,128)(2,1)S(1)} %coefficients.1.refs_0_), channel_id=1, source_target_pairs={{0,16},{1,17},{2,18},{3,19},{4,20},{5,21},{6,22},{7,23},{8,24},{9,... | collective-permute-start | bytes 614408 | tf_op jit(solution)/shard_map/ppermute | solution.py:32
  13.5 10.3 %collective-permute-start.2 = (bf16[800,128]{1,0:T(8,128)(2,1)S(1)}, bf16[800,128]{1,0:T(8,128)(2,1)S(1)}, u32[]{:S(2)}, u32[]{:S(2)}) collective-permute-start(bf16[800,128]{1,0:T(8,128)(2,1)S(1)} %coefficients.1.refs_0_), channel_id=1, source_target_pairs={{0,8},{1,9},{2,10},{3,11},{4,12},{5,13},{6,14},{7,15},{8,16},{9,17... | collective-permute-start | bytes 614408 | tf_op jit(solution)/shard_map/ppermute | solution.py:32
  13.5 10.3 %collective-permute-start.3 = (bf16[800,128]{1,0:T(8,128)(2,1)S(1)}, bf16[800,128]{1,0:T(8,128)(2,1)S(1)}, u32[]{:S(2)}, u32[]{:S(2)}) collective-permute-start(bf16[800,128]{1,0:T(8,128)(2,1)S(1)} %coefficients.1.refs_0_), channel_id=1, source_target_pairs={{0,24},{1,25},{2,26},{3,27},{4,28},{5,29},{6,30},{7,31},{8,0},{9,1... | collective-permute-start | bytes 614408 | tf_op jit(solution)/shard_map/ppermute | solution.py:32
  15.6 8.8 %collective-permute-start.8 = (bf16[306,256]{1,0:T(8,128)(2,1)S(1)}, bf16[306,256]{1,0:T(8,128)(2,1)S(1)}, u32[]{:S(2)}, u32[]{:S(2)}) collective-permute-start(bf16[306,256]{1,0:T(8,128)(2,1)S(1)} %collective-permute-done.7.refs_8_), channel_id=1, source_target_pairs={{0,32},{1,33},{2,34},{3,35},{4,36},{5,37},{6,38},{7,39},{8,40},{9,... | collective-permute-start | bytes 470024 | tf_op jit(solution)/shard_map/ppermute | solution.py:32
  15.6 10.7 %collective-permute-start = (bf16[800,128]{1,0:T(8,128)(2,1)S(1)}, bf16[800,128]{1,0:T(8,128)(2,1)S(1)}, u32[]{:S(2)}, u32[]{:S(2)}) collective-permute-start(bf16[800,128]{1,0:T(8,128)(2,1)S(1)} %coefficients.1.refs_0_), channel_id=1, source_target_pairs={{0,1},{1,0},{2,3},{3,2},{4,5},{5,4},{6,7},{7,6},{8,9},{9,8},{10,11... | collective-permute-start | bytes 614408 | tf_op jit(solution)/shard_map/ppermute | solution.py:32
  20.7 6.0 %collective-permute-start.4 = (bf16[800,128]{1,0:T(8,128)(2,1)S(1)}, bf16[800,128]{1,0:T(8,128)(2,1)S(1)}, u32[]{:S(2)}, u32[]{:S(2)}) collective-permute-start(bf16[800,128]{1,0:T(8,128)(2,1)S(1)} %collective-permute-done.1.refs_0_), channel_id=1, source_target_pairs={{0,1},{1,0},{2,3},{3,2},{4,5},{5,4},{6,7},{7,6},{8,9},{9,8},{10,11... | collective-permute-start | bytes 614408 | tf_op jit(solution)/shard_map/ppermute | solution.py:32
  23.8 3.3 %collective-permute-start.5 = (bf16[800,128]{1,0:T(8,128)(2,1)S(1)}, bf16[800,128]{1,0:T(8,128)(2,1)S(1)}, u32[]{:S(2)}, u32[]{:S(2)}) collective-permute-start(bf16[800,128]{1,0:T(8,128)(2,1)S(1)} %collective-permute-done.2.refs_0_), channel_id=1, source_target_pairs={{0,1},{1,0},{2,3},{3,2},{4,5},{5,4},{6,7},{7,6},{8,9},{9,8},{10,11... | collective-permute-start | bytes 614408 | tf_op jit(solution)/shard_map/ppermute | solution.py:32
  23.8 3.7 %collective-permute-start.6 = (bf16[800,128]{1,0:T(8,128)(2,1)S(1)}, bf16[800,128]{1,0:T(8,128)(2,1)S(1)}, u32[]{:S(2)}, u32[]{:S(2)}) collective-permute-start(bf16[800,128]{1,0:T(8,128)(2,1)S(1)} %collective-permute-done.3.refs_0_), channel_id=1, source_target_pairs={{0,1},{1,0},{2,3},{3,2},{4,5},{5,4},{6,7},{7,6},{8,9},{9,8},{10,11... | collective-permute-start | bytes 614408 | tf_op jit(solution)/shard_map/ppermute | solution.py:32
  24.3 11.0 %collective-permute-start.9 = (bf16[306,256]{1,0:T(8,128)(2,1)S(1)}, bf16[306,256]{1,0:T(8,128)(2,1)S(1)}, u32[]{:S(2)}, u32[]{:S(2)}) collective-permute-start(bf16[306,256]{1,0:T(8,128)(2,1)S(1)} %collective-permute-done.8.refs_8_), channel_id=1, source_target_pairs={{0,38},{1,39},{2,32},{3,33},{4,34},{5,35},{6,36},{7,37},{8,46},{9,... | collective-permute-start | bytes 470024 | tf_op jit(solution)/shard_map/ppermute | solution.py:32
  29.4 13.1 %collective-permute-start.12 = (bf16[256,256]{1,0:T(8,128)(2,1)S(1)}, bf16[256,256]{1,0:T(8,128)(2,1)S(1)}, u32[]{:S(2)}, u32[]{:S(2)}) collective-permute-start(bf16[256,256]{1,0:T(8,128)(2,1)S(1)} %partials.7), channel_id=1, source_target_pairs={{0,2},{1,3},{2,4},{3,5},{4,6},{5,7},{6,0},{7,1},{8,10},{9,11},{10,... | collective-permute-start | bytes 393224 | tf_op jit(solution)/shard_map/ppermute | solution.py:32
  31.1 10.0 %copy-start.1 = (bf16[256,306]{0,1:T(8,128)(2,1)S(1)}, bf16[256,306]{0,1:T(8,128)(2,1)}, u32[]{:S(2)}) copy-start(bf16[256,306]{0,1:T(8,128)(2,1)} %param.4) | copy-start | bytes 470020
  31.1 11.3 %collective-permute-start.11 = (bf16[256,256]{1,0:T(8,128)(2,1)S(1)}, bf16[256,256]{1,0:T(8,128)(2,1)S(1)}, u32[]{:S(2)}, u32[]{:S(2)}) collective-permute-start(bf16[256,256]{1,0:T(8,128)(2,1)S(1)} %partials.6), channel_id=1, source_target_pairs={{0,6},{1,7},{2,0},{3,1},{4,2},{5,3},{6,4},{7,5},{8,14},{9,15},{10,... | collective-permute-start | bytes 393224 | tf_op jit(solution)/shard_map/ppermute | solution.py:32
  36.8 11.6 %collective-permute-start.10 = (bf16[256,256]{1,0:T(8,128)(2,1)S(1)}, bf16[256,256]{1,0:T(8,128)(2,1)S(1)}, u32[]{:S(2)}, u32[]{:S(2)}) collective-permute-start(bf16[256,256]{1,0:T(8,128)(2,1)S(1)} %partials.5), channel_id=1, source_target_pairs={{0,4},{1,5},{2,6},{3,7},{4,0},{5,1},{6,2},{7,3},{8,12},{9,13},{10,... | collective-permute-start | bytes 393224 | tf_op jit(solution)/shard_map/ppermute | solution.py:32
